TPU v7x, 32 devices: a whole 2x2x4 slice. The times are simulated.
32 devices in a mesh: seq: 8 (over y, x, core), grp: 4 (over z).
Axes of the slice: x: 2, y: 2, z: 4, core: 2. Of those that a mesh axis runs over, the one named last changes fastest.
Arguments:
- byte_ids: int32 [1536, 8], P('seq'), may hold values from 0 to 255
- patch_order: int32 [1536], P('seq'), may hold values from 0 to 1535, as said below
- query_rows: bfloat16 [1536, 8192], P('seq', 'grp'), may hold values from -25 to 25
- key_rows: bfloat16 [1536, 8192], P('seq', 'grp'), may hold values from -25 to 25
- value_rows: bfloat16 [1536, 8192], P('seq', 'grp'), may hold values from -6 to 6
- byte_embed: bfloat16 [256, 1024], replicated, may hold values from -6.5 to 6.5
- norm_gain: float32 [1024], replicated, may hold values from 0.25 to 1.75
- w_up: bfloat16 [1024, 4096], replicated, may hold values from -0.1875 to 0.1875
- w_down: bfloat16 [4096, 1024], replicated, may hold values from -0.09375 to 0.09375
- vocab_head: bfloat16 [1024, 256], replicated, may hold values from -12 to 12
Outputs:
- byte_loss: float32 [1536, 8], P(('seq', 'grp'))
- query_grad: bfloat16 [1536, 8192], P('seq', 'grp')
- key_grad: bfloat16 [1536, 8192], P('seq', 'grp')
- value_grad: bfloat16 [1536, 8192], P('seq', 'grp')
Inputs may be any that keep to these rules, and one draw needn't show every extreme that they name: `patch_order`: each aligned block of 192 entries is a permutation of that block's own indices.
All inputs are finite; a program needn't handle non-finite values.
Results may differ from a plain program's by a relative error of at most 0.028.
Values may be sent and summed in bfloat16 or wider, within the bound.
A program may use at most 192 MiB of HBM per device.

v0:
```python
import functools

import jax
import jax.numpy as jnp
from jax import lax
from jax.experimental import pallas as pl
from jax.experimental.pallas import tpu as pltpu
from jax.sharding import PartitionSpec as P

HEAD = 128
PATCH = 8


EPSILON = 1e-05
FLOOR = -1e30


def shortened(value):
    return jax.tree.map(lambda a: a.astype(jnp.bfloat16) if a.dtype == jnp.float32 else a, value)


def partner_2(value, axis, bit):
    mask = 2**bit
    pairs = [(source, source ^ mask) for source in range(lax.axis_size(axis))]
    return lax.ppermute(value, axis, pairs)


def local_model(context, byte_ids, byte_embed, norm_gain, w_up, w_down, vocab_head):
    patch_count = context.shape[0]
    model_width = byte_embed.shape[1]
    vocab_size = vocab_head.shape[1]
    hidden_in = context.astype(jnp.float32).reshape(patch_count * PATCH, model_width)
    previous = jnp.concatenate([byte_ids[:, :1], byte_ids[:, :-1]], axis=1).reshape(-1)
    live_rows = jnp.tile(jnp.arange(PATCH) > 0, patch_count)
    letters = jnp.arange(vocab_size)
    one_hot = ((previous[:, None] == letters[None, :]) & live_rows[:, None]).astype(jnp.bfloat16)
    hidden_in = hidden_in + jnp.dot(one_hot, byte_embed, preferred_element_type=jnp.float32)
    inverse_rms = lax.rsqrt(jnp.mean(hidden_in * hidden_in, axis=1, keepdims=True) + EPSILON)
    normed = (hidden_in * inverse_rms * norm_gain).astype(jnp.bfloat16)
    raised = jnp.dot(normed, w_up, preferred_element_type=jnp.float32)
    active = jax.nn.gelu(raised, approximate=True).astype(jnp.bfloat16)
    after_mlp = hidden_in + jnp.dot(active, w_down, preferred_element_type=jnp.float32)
    final_scale = lax.rsqrt(jnp.mean(after_mlp * after_mlp, axis=1, keepdims=True) + EPSILON)
    final_rows = (after_mlp * final_scale).astype(jnp.bfloat16)
    logits = jnp.dot(final_rows, vocab_head, preferred_element_type=jnp.float32)
    row_top = lax.stop_gradient(jnp.max(logits, axis=1, keepdims=True))
    log_total = jnp.log(jnp.sum(jnp.exp(logits - row_top), axis=1)) + row_top[:, 0]
    target = byte_ids.reshape(-1)
    chosen = jnp.sum(jnp.where(target[:, None] == letters[None, :], logits, 0.0), axis=1)
    return (log_total - chosen).reshape(patch_count, PATCH)


def head_order(flat, head_count, segments, seq_count):
    row_total = flat.shape[0]
    block_rows = row_total // segments
    arranged = flat.reshape(block_rows, segments, head_count, HEAD).transpose(2, 1, 0, 3)
    return arranged.reshape(seq_count, -1, block_rows, HEAD)


def row_order(stack, head_count, segments):
    block_rows = stack.shape[2]
    arranged = stack.reshape(head_count, segments, block_rows, HEAD).transpose(2, 1, 0, 3)
    return arranged.reshape(block_rows * segments, head_count * HEAD)


def shards(
    byte_ids,
    patch_order,
    query_rows,
    key_rows,
    value_rows,
    byte_embed,
    norm_gain,
    w_up,
    w_down,
    vocab_head,
):
    row_count = query_rows.shape[0]
    head_count = query_rows.shape[1] // HEAD
    seq_here = lax.axis_index("seq")
    grp_here = lax.axis_index("grp")
    first_here = seq_here * row_count
    seq_count = lax.axis_size("seq")
    segments = max(1, seq_count // head_count)
    held_heads = max(1, head_count // seq_count)
    bit_count = segments.bit_length() - 1
    residue = seq_here % segments
    arranged = tuple(
        (
            head_order(member, head_count, segments, seq_count)
            for member in (query_rows, key_rows, value_rows)
        )
    )
    own_query, own_key, own_value = jax.tree.map(
        lambda part, own: part.astype(own.dtype),
        lax.all_to_all(shortened(arranged), "seq", split_axis=0, concat_axis=2, tiled=True),
        arranged,
    )
    stacked = jnp.stack([own_key, own_value])
    for bit in range(bit_count):
        partner = partner_2(shortened(stacked), "seq", bit).astype(stacked.dtype)
        upper_half = seq_here >> bit & 1 == 1
        stacked = jnp.where(
            upper_half,
            jnp.concatenate([partner, stacked], 1),
            jnp.concatenate([stacked, partner], 1),
        )
    slot_count = own_query.shape[2]
    full_pairs = stacked.transpose(0, 2, 3, 1, 4).reshape(
        2, held_heads, slot_count * segments, HEAD
    )
    full_key = full_pairs[0]
    full_value = full_pairs[1]
    head_queries = own_query[0]
    query_pos = jnp.arange(slot_count, dtype=jnp.int32) * segments + residue
    key_pos = jnp.arange(slot_count * segments, dtype=jnp.int32)
    allowed = (key_pos[None, :] <= query_pos[:, None])[None]
    scores = jnp.einsum(
        "hqd,hkd->hqk", head_queries, full_key, preferred_element_type=jnp.float32
    ) * HEAD ** (-0.5)
    row_top = jnp.max(jnp.where(allowed, scores, FLOOR), axis=2, keepdims=True)
    spread = jnp.where(allowed, jnp.exp(jnp.where(allowed, scores - row_top, FLOOR)), 0.0)
    head_mass = row_top[:, :, 0] + jnp.log(jnp.sum(spread, axis=2))
    chances = jnp.where(
        allowed, jnp.exp(jnp.where(allowed, scores - head_mass[:, :, None], FLOOR)), 0.0
    )
    rounded_weights = chances.astype(jnp.bfloat16)
    head_attended = jnp.einsum(
        "hqk,hkd->hqd", chances, full_value.astype(jnp.float32), precision=lax.Precision.HIGHEST
    ).astype(jnp.bfloat16)
    attended = row_order(
        lax.all_to_all(head_attended[None], "seq", split_axis=2, concat_axis=0, tiled=True),
        head_count,
        segments,
    )
    local_order = patch_order - first_here
    ordered = jnp.take(attended, local_order, axis=0)
    owned_rows = lax.all_to_all(ordered, "grp", split_axis=0, concat_axis=1, tiled=True)
    group_rows = owned_rows.shape[0]
    slot_patches = lax.dynamic_slice_in_dim(local_order, grp_here * group_rows, group_rows, 0)
    slot_bytes = jnp.take(byte_ids, slot_patches, axis=0)

    def scored(context):
        return local_model(context, slot_bytes, byte_embed, norm_gain, w_up, w_down, vocab_head)

    byte_loss, pull_back = jax.vjp(scored, owned_rows)
    (context_grad,) = pull_back(jnp.ones_like(byte_loss))
    returned = lax.all_to_all(context_grad, "grp", split_axis=1, concat_axis=0, tiled=True)
    grads_flat = jnp.zeros_like(returned).at[local_order].set(returned)
    arranged_grads = head_order(grads_flat, head_count, segments, seq_count)
    grad_heads = lax.all_to_all(arranged_grads, "seq", split_axis=0, concat_axis=2, tiled=True)[0]
    head_dot = jnp.sum(grad_heads.astype(jnp.float32) * head_attended.astype(jnp.float32), axis=2)
    chance_grad = jnp.einsum(
        "hqd,hkd->hqk", grad_heads, full_value, preferred_element_type=jnp.float32
    )
    score_grad = (chances * (chance_grad - head_dot[:, :, None])).astype(jnp.bfloat16)
    query_heads = (
        jnp.einsum("hqk,hkd->hqd", score_grad, full_key, preferred_element_type=jnp.float32)
        * HEAD ** (-0.5)
    ).astype(jnp.bfloat16)
    key_part = jnp.einsum(
        "hqk,hqd->hkd", score_grad, head_queries, preferred_element_type=jnp.float32
    ) * HEAD ** (-0.5)
    value_part = jnp.einsum(
        "hqk,hqd->hkd", rounded_weights, grad_heads, preferred_element_type=jnp.float32
    )
    partial_pairs = (
        jnp.stack([key_part, value_part])
        .reshape(2, held_heads, slot_count, segments, HEAD)
        .transpose(0, 3, 1, 2, 4)
    )
    for bit in reversed(range(bit_count)):
        half_count = partial_pairs.shape[1] // 2
        upper_half = seq_here >> bit & 1 == 1
        lower_part = partial_pairs[:, :half_count]
        upper_part = partial_pairs[:, half_count:]
        kept_half = jnp.where(upper_half, upper_part, lower_part)
        sent_half = jnp.where(upper_half, lower_part, upper_part)
        partial_pairs = kept_half + partner_2(sent_half.astype(jnp.bfloat16), "seq", bit).astype(
            sent_half.dtype
        )
    key_heads = partial_pairs[0].astype(jnp.bfloat16)
    value_heads = partial_pairs[1].astype(jnp.bfloat16)
    back_query, back_key, back_value = (
        lax.all_to_all(query_heads[None], "seq", split_axis=2, concat_axis=0, tiled=True),
        lax.all_to_all(key_heads, "seq", split_axis=2, concat_axis=0, tiled=True),
        lax.all_to_all(value_heads, "seq", split_axis=2, concat_axis=0, tiled=True),
    )
    query_out = row_order(back_query, head_count, segments)
    key_out = row_order(back_key, head_count, segments)
    value_out = row_order(back_value, head_count, segments)
    return (byte_loss, query_out, key_out, value_out)


MESH = pl.DeviceIdType.MESH
LANES = 128
KEY_TILE = 256
HIDDEN_TILE = 512
GELU_A = 0.7978845608028654
GELU_B = 0.044715
LOG2E = 1.4426950408889634
SCALE = HEAD ** (-0.5)


def dot_nn(a, b):
    return lax.dot_general(a, b, (((1,), (0,)), ((), ())), preferred_element_type=jnp.float32)


def dot_nt(a, b):
    return lax.dot_general(a, b, (((1,), (1,)), ((), ())), preferred_element_type=jnp.float32)


def dot_tn(a, b):
    return lax.dot_general(a, b, (((0,), (0,)), ((), ())), preferred_element_type=jnp.float32)


def fused_kernel(
    seq_count,
    grp_count,
    ids_ref,
    gain_ref,
    q_in,
    k_in,
    v_in,
    embed_in,
    up_in,
    down_in,
    vocab_in,
    loss_out,
    dq_out,
    dk_out,
    dv_out,
    q_buf,
    k_buf,
    v_buf,
    p_buf,
    att,
    ctx,
    dctx,
    dout,
    dq_buf,
    dk_buf,
    dv_buf,
    embed,
    up,
    down,
    vocab,
    hid,
    normed,
    slope,
    acc,
    dafter,
    dafter_low,
    loss_mine,
    in_recv,
    in_send,
    weight_sem,
    ctx_recv,
    ctx_send,
    grad_recv,
    grad_send,
    loss_recv,
    loss_send,
    loss_local,
    out_recv,
    out_send,
):
    me_s = lax.axis_index("seq")
    me_g = lax.axis_index("grp")
    devices = seq_count * grp_count
    me = me_s * grp_count + me_g
    total, width = q_buf.shape
    rows = total // seq_count
    heads = width // HEAD
    part = rows // grp_count
    model = embed.shape[1]
    vocab_size = embed.shape[0]
    ffl = up.shape[1]
    slots = part * PATCH

    weight_copies = [
        pltpu.make_async_copy(a, b, weight_sem.at[n])
        for n, (a, b) in enumerate(
            ((embed_in, embed), (vocab_in, vocab), (up_in, up), (down_in, down))
        )
    ]
    for copy in weight_copies:
        copy.start()

    barrier = pltpu.get_barrier_semaphore()

    def greet(d, _):
        peer = lax.rem(me + d, devices)
        pl.semaphore_signal(
            barrier,
            inc=1,
            device_id=(peer // grp_count, lax.rem(peer, grp_count)),
            device_id_type=MESH,
        )
        return 0

    lax.fori_loop(1, devices, greet, 0)
    my_rows = pl.ds(pl.multiple_of(me_s * rows, rows), rows)
    my_cols = pl.ds(pl.multiple_of(me_s * width, width), width)
    arrays = ((k_in, k_buf), (q_in, q_buf), (v_in, v_buf))
    for n, (source, target) in enumerate(arrays):
        pltpu.make_async_copy(source.at[:, my_cols], target.at[my_rows], in_recv.at[n]).start()
    pl.semaphore_wait(barrier, devices - 1)

    for n, (source, target) in enumerate(arrays):

        def send_in(d, _, n=n, source=source, target=target):
            peer = lax.rem(me_s + d, seq_count)
            pltpu.make_async_remote_copy(
                src_ref=source.at[:, pl.ds(pl.multiple_of(peer * width, width), width)],
                dst_ref=target.at[my_rows],
                send_sem=in_send.at[n],
                recv_sem=in_recv.at[n],
                device_id=(peer, me_g),
                device_id_type=MESH,
            ).start()
            return 0

        lax.fori_loop(1, seq_count, send_in, 0)

    my_ids = ids_ref[pl.ds(pl.multiple_of(me_g * part, part), part), :]
    letters = lax.broadcasted_iota(jnp.int32, (part, vocab_size), 1)
    weight_copies[0].wait()
    hid[:part, :] = jnp.zeros((part, model), jnp.float32)
    for t in range(1, PATCH):
        one_hot = (my_ids[:, t - 1 : t] == letters).astype(jnp.bfloat16)
        hid[t * part : (t + 1) * part, :] = dot_nn(one_hot, embed[...])

    widths = [-(-((i + 1) * rows) // KEY_TILE) * KEY_TILE for i in range(seq_count)]

    def head_cols(h):
        return pl.ds(pl.multiple_of(h * HEAD, HEAD), HEAD)

    def wait_in(n):
        target = arrays[n][1]
        pltpu.make_async_copy(target, target, in_recv.at[n]).wait()

    wait_in(0)
    wait_in(1)

    def weigh(h, _):
        cols = head_cols(h)
        for i, w in enumerate(widths):
            start = i * rows // LANES * LANES
            s = dot_nt(q_buf[i * rows : (i + 1) * rows, cols], k_buf[:w, cols])
            tail = s[:, start:]
            key_pos = lax.broadcasted_iota(jnp.int32, tail.shape, 1) + start
            query_pos = lax.broadcasted_iota(jnp.int32, tail.shape, 0) + i * rows
            tail = jnp.where(key_pos <= query_pos, tail, FLOOR)
            if start:
                s = jnp.concatenate([s[:, :start], tail], axis=1)
            else:
                s = tail
            top = jnp.max(s, axis=1, keepdims=True)
            e = jnp.exp2((s - top) * (SCALE * LOG2E))
            inverse = 1.0 / jnp.sum(e, axis=1, keepdims=True)
            p_buf[h, i * rows : (i + 1) * rows, :w] = (e * inverse).astype(jnp.bfloat16)
        return 0

    lax.fori_loop(0, heads, weigh, 0)
    wait_in(2)

    first_col = (me_g * seq_count + me_s) * width

    def attend(h, _):
        cols = head_cols(h)
        for i, w in enumerate(widths):
            block = dot_nn(p_buf[h, i * rows : (i + 1) * rows, :w], v_buf[:w, cols])
            att[i * rows : (i + 1) * rows, cols] = block.astype(jnp.bfloat16)
        there = pl.ds(pl.multiple_of(first_col + h * HEAD, HEAD), HEAD)

        def send_ctx(d, _):
            peer = lax.rem(me + d, devices)
            pltpu.make_async_remote_copy(
                src_ref=att.at[pl.ds(pl.multiple_of(peer * part, part), part), cols],
                dst_ref=ctx.at[:, there],
                send_sem=ctx_send,
                recv_sem=ctx_recv,
                device_id=(peer // grp_count, lax.rem(peer, grp_count)),
                device_id_type=MESH,
            ).start()
            return 0

        lax.fori_loop(1, devices, send_ctx, 0)
        ctx[:, there] = att[pl.ds(pl.multiple_of(me * part, part), part), cols]
        return 0

    lax.fori_loop(0, heads, attend, 0)
    others = ctx.at[:, : (devices - 1) * width]
    pltpu.make_async_copy(others, others, ctx_recv).wait()

    for t in range(PATCH):
        hid[t * part : (t + 1) * part, :] += ctx[:, t * model : (t + 1) * model].astype(jnp.float32)
    h0 = hid[...]
    inverse_rms = lax.rsqrt(jnp.mean(h0 * h0, axis=1, keepdims=True) + EPSILON)
    normed[...] = (h0 * inverse_rms * gain_ref[...]).astype(jnp.bfloat16)
    acc[...] = h0
    for copy in weight_copies[1:]:
        copy.wait()

    def raise_step(c, _):
        chunk = pl.ds(pl.multiple_of(c * HIDDEN_TILE, HIDDEN_TILE), HIDDEN_TILE)
        x = dot_nn(normed[...], up[:, chunk])
        square = x * x
        th = jnp.tanh(x * (GELU_A + (GELU_A * GELU_B) * square))
        half = 0.5 + 0.5 * th
        active = (x * half).astype(jnp.bfloat16)
        slope[:, chunk] = half + (0.5 * x) * (1.0 - th * th) * (
            GELU_A + (3.0 * GELU_A * GELU_B) * square
        )
        acc[...] += dot_nn(active, down[chunk, :])
        return 0

    lax.fori_loop(0, ffl // HIDDEN_TILE, raise_step, 0)
    after = acc[...]
    final_scale = lax.rsqrt(jnp.mean(after * after, axis=1, keepdims=True) + EPSILON)
    final_rows = (after * final_scale).astype(jnp.bfloat16)
    logits = dot_nn(final_rows, vocab[...])
    top = jnp.max(logits, axis=1, keepdims=True)
    e = jnp.exp(logits - top)
    z = jnp.sum(e, axis=1, keepdims=True)
    hot = jnp.concatenate(
        [(my_ids[:, t : t + 1] == letters).astype(jnp.float32) for t in range(PATCH)], axis=0
    )
    loss = jnp.log(z) + top - jnp.sum(hot * logits, axis=1, keepdims=True)
    lane = lax.broadcasted_iota(jnp.int32, (part, LANES), 1)
    tile = jnp.zeros((part, LANES), jnp.float32)
    for t in range(PATCH):
        tile = jnp.where(lane == t, loss[t * part : (t + 1) * part, :], tile)
    loss_mine[...] = tile
    loss_place = loss_out.at[pl.ds(pl.multiple_of(me_g * part, part), part), :]
    loss_copy = pltpu.make_async_copy(loss_mine, loss_place, loss_local)
    loss_copy.start()

    def send_loss(d, _):
        pltpu.make_async_remote_copy(
            src_ref=loss_mine,
            dst_ref=loss_place,
            send_sem=loss_send,
            recv_sem=loss_recv,
            device_id=(me_s, lax.rem(me_g + d, grp_count)),
            device_id_type=MESH,
        ).start()
        return 0

    lax.fori_loop(1, grp_count, send_loss, 0)
    dlogits = (e / z - hot).astype(jnp.bfloat16)
    dfinal = dot_nt(dlogits, vocab[...]).astype(jnp.bfloat16).astype(jnp.float32)
    after = acc[...]
    share = jnp.mean(dfinal * after, axis=1, keepdims=True)
    da = final_scale * dfinal - after * (final_scale * final_scale * final_scale * share)
    dafter[...] = da
    dafter_low[...] = da.astype(jnp.bfloat16)
    acc[...] = jnp.zeros_like(acc)

    def lower_step(c, _):
        chunk = pl.ds(pl.multiple_of(c * HIDDEN_TILE, HIDDEN_TILE), HIDDEN_TILE)
        dactive = dot_nt(dafter_low[...], down[chunk, :]).astype(jnp.bfloat16)
        draised = (dactive.astype(jnp.float32) * slope[:, chunk]).astype(jnp.bfloat16)
        acc[...] += dot_nt(draised, up[:, chunk])
        return 0

    lax.fori_loop(0, ffl // HIDDEN_TILE, lower_step, 0)
    dn = acc[...].astype(jnp.bfloat16).astype(jnp.float32) * gain_ref[...]
    h0 = hid[...]
    share = jnp.mean(dn * h0, axis=1, keepdims=True)
    dh = inverse_rms * dn - h0 * (inverse_rms * inverse_rms * inverse_rms * share) + dafter[...]
    for t in range(PATCH):
        dctx[:, t * model : (t + 1) * model] = dh[t * part : (t + 1) * part, :].astype(jnp.bfloat16)

    my_part = pl.ds(pl.multiple_of(me * part, part), part)

    def send_grad(d, _):
        peer = lax.rem(me + d, devices)
        peer_s = peer // grp_count
        peer_g = lax.rem(peer, grp_count)
        from_col = (peer_g * seq_count + peer_s) * width
        pltpu.make_async_remote_copy(
            src_ref=dctx.at[:, pl.ds(pl.multiple_of(from_col, width), width)],
            dst_ref=dout.at[my_part, :],
            send_sem=grad_send,
            recv_sem=grad_recv,
            device_id=(peer_s, peer_g),
            device_id_type=MESH,
        ).start()
        return 0

    lax.fori_loop(1, devices, send_grad, 0)
    dout[my_part, :] = dctx[:, pl.ds(pl.multiple_of(first_col, width), width)]
    others = dout.at[: (devices - 1) * part, :]
    pltpu.make_async_copy(others, others, grad_recv).wait()

    def send_out(n, source, target):
        pltpu.make_async_copy(source.at[my_rows, :], target.at[:, my_cols], out_recv.at[n]).start()

        def send_one(d, _):
            peer = lax.rem(me_s + d, seq_count)
            pltpu.make_async_remote_copy(
                src_ref=source.at[pl.ds(pl.multiple_of(peer * rows, rows), rows), :],
                dst_ref=target.at[:, my_cols],
                send_sem=out_send.at[n],
                recv_sem=out_recv.at[n],
                device_id=(peer, me_g),
                device_id_type=MESH,
            ).start()
            return 0

        lax.fori_loop(1, seq_count, send_one, 0)

    def key_side(matrix, side, result, factor):
        def one_head(h, _):
            cols = head_cols(h)
            for c in range(total // KEY_TILE):
                first = next(i for i, w in enumerate(widths) if w >= (c + 1) * KEY_TILE) * rows
                block = dot_tn(
                    matrix[h, first:, c * KEY_TILE : (c + 1) * KEY_TILE], side[first:, cols]
                )
                if factor is not None:
                    block = block * factor
                result[c * KEY_TILE : (c + 1) * KEY_TILE, cols] = block.astype(jnp.bfloat16)
            return 0

        lax.fori_loop(0, heads, one_head, 0)

    key_side(p_buf, dout, dv_buf, None)
    send_out(2, dv_buf, dv_out)

    def query_side(h, _):
        cols = head_cols(h)
        for i, w in enumerate(widths):
            here = slice(i * rows, (i + 1) * rows)
            g = dout[here, cols]
            row_dot = jnp.sum(
                g.astype(jnp.float32) * att[here, cols].astype(jnp.float32), axis=1, keepdims=True
            )
            dp = dot_nt(g, v_buf[:w, cols])
            ds = (p_buf[h, here, :w].astype(jnp.float32) * (dp - row_dot)).astype(jnp.bfloat16)
            p_buf[h, here, :w] = ds
            dq_buf[here, cols] = (dot_nn(ds, k_buf[:w, cols]) * SCALE).astype(jnp.bfloat16)
        return 0

    lax.fori_loop(0, heads, query_side, 0)
    send_out(0, dq_buf, dq_out)
    key_side(p_buf, q_buf, dk_buf, SCALE)
    send_out(1, dk_buf, dk_out)

    loss_copy.wait()
    loss_others = loss_out.at[: (grp_count - 1) * part, :]
    pltpu.make_async_copy(loss_others, loss_others, loss_recv).wait()
    pltpu.make_async_copy(loss_others, loss_others, loss_send).wait()
    sent = q_in.at[:, : (seq_count - 1) * width]
    for n in range(3):
        pltpu.make_async_copy(sent, sent, in_send.at[n]).wait()
    others = ctx.at[:, : (devices - 1) * width]
    pltpu.make_async_copy(others, others, ctx_send).wait()
    pltpu.make_async_copy(others, others, grad_send).wait()
    for n, target in enumerate((dq_out, dk_out, dv_out)):
        pltpu.make_async_copy(target, target, out_recv.at[n]).wait()
        others = target.at[:, : (seq_count - 1) * width]
        pltpu.make_async_copy(others, others, out_send.at[n]).wait()


def fits(seq_count, grp_count, byte_ids, patch_order, query_rows, *rest):
    rows, columns = query_rows.shape
    model = rest[2].shape[1]
    ffl = rest[4].shape[1]
    total = rows * seq_count
    heads = columns // HEAD
    return (
        heads % seq_count == 0
        and rows % (16 * grp_count) == 0
        and total % KEY_TILE == 0
        and ffl % HIDDEN_TILE == 0
        and columns * grp_count == model * PATCH
        and (heads // seq_count) * total * total <= 6 * 1024 * 1024
    )


def fused_shards(
    seq_count,
    grp_count,
    byte_ids,
    patch_order,
    query_rows,
    key_rows,
    value_rows,
    byte_embed,
    norm_gain,
    w_up,
    w_down,
    vocab_head,
):
    rows, columns = query_rows.shape
    width = columns // seq_count
    total = rows * seq_count
    part = rows // grp_count
    heads = width // HEAD
    vocab_size, model = byte_embed.shape
    ffl = w_up.shape[1]
    slots = part * PATCH
    low, wide = jnp.bfloat16, jnp.float32
    anywhere = pl.BlockSpec(memory_space=pl.ANY)
    inside = pl.BlockSpec(memory_space=pltpu.VMEM)
    grad_shape = jax.ShapeDtypeStruct((rows, columns), low)
    dma = pltpu.SemaphoreType.DMA
    losses, query_grad, key_grad, value_grad = pl.pallas_call(
        functools.partial(fused_kernel, seq_count, grp_count),
        out_shape=(
            jax.ShapeDtypeStruct((rows, LANES), wide),
            grad_shape,
            grad_shape,
            grad_shape,
        ),
        in_specs=[inside] * 2 + [anywhere] * 7,
        out_specs=(anywhere,) * 4,
        scratch_shapes=[
            pltpu.VMEM((total, width), low),
            pltpu.VMEM((total, width), low),
            pltpu.VMEM((total, width), low),
            pltpu.VMEM((heads, total, total), low),
            pltpu.VMEM((total, width), low),
            pltpu.VMEM((part, PATCH * model), low),
            pltpu.VMEM((part, PATCH * model), low),
            pltpu.VMEM((total, width), low),
            pltpu.VMEM((total, width), low),
            pltpu.VMEM((total, width), low),
            pltpu.VMEM((total, width), low),
            pltpu.VMEM((vocab_size, model), low),
            pltpu.VMEM((model, ffl), low),
            pltpu.VMEM((ffl, model), low),
            pltpu.VMEM((model, vocab_size), low),
            pltpu.VMEM((slots, model), wide),
            pltpu.VMEM((slots, model), low),
            pltpu.VMEM((slots, ffl), wide),
            pltpu.VMEM((slots, model), wide),
            pltpu.VMEM((slots, model), wide),
            pltpu.VMEM((slots, model), low),
            pltpu.VMEM((part, LANES), wide),
            dma((3,)),
            dma((3,)),
            dma((4,)),
            dma,
            dma,
            dma,
            dma,
            dma,
            dma,
            dma,
            dma((3,)),
            dma((3,)),
        ],
        compiler_params=pltpu.CompilerParams(
            collective_id=0, has_side_effects=True, vmem_limit_bytes=67_000_000
        ),
    )(
        byte_ids,
        norm_gain.reshape(1, model),
        query_rows,
        key_rows,
        value_rows,
        byte_embed,
        w_up,
        w_down,
        vocab_head,
    )
    first_here = lax.axis_index("seq") * rows
    local_order = patch_order - first_here
    mine = lax.dynamic_slice_in_dim(local_order, lax.axis_index("grp") * part, part, 0)
    chosen = (mine[:, None] == jnp.arange(rows)[None, :]).astype(wide)
    byte_loss = jnp.dot(chosen, losses, precision=lax.Precision.HIGHEST)[:, :PATCH]
    return byte_loss, query_grad, key_grad, value_grad


def solution(mesh):
    placed = (
        P("seq", None),
        P("seq"),
        P("seq", "grp"),
        P("seq", "grp"),
        P("seq", "grp"),
        P(),
        P(),
        P(),
        P(),
        P(),
    )
    seq_count, grp_count = mesh.shape["seq"], mesh.shape["grp"]

    def body(*args):
        if fits(seq_count, grp_count, *args):
            return fused_shards(seq_count, grp_count, *args)
        return shards(*args)

    return jax.shard_map(
        body,
        mesh=mesh,
        in_specs=placed,
        out_specs=(P(("seq", "grp"), None), P("seq", "grp"), P("seq", "grp"), P("seq", "grp")),
        check_vma=False,
    )
```

profile of v0, /device:TPU:1, one launch (start us, length us, event | category | flops | bytes accessed | tf_op | source)
XLA Modules:
  0.0 134.7 jit_solution(12444064400098545453)
XLA Ops:
  0.6 0.7 broadcast_subtract_fusion
  1.3 0.1 dynamic_slice.3
  1.4 1.5 %copy.14.ids_ref = s32[192,8]{1,0:T(8,128)} copy(s32[192,8]{0,1:T(8,128)} %param.10) | data formatting | bytes 12288 | tf_op args[0]
  2.8 123.8 %shard_map.129 = (f32[192,128]{1,0:T(8,128)}, bf16[192,2048]{1,0:T(8,128)(2,1)}, bf16[192,2048]{1,0:T(8,128)(2,1)}, bf16[192,2048]{1,0:T(8,128)(2,1)}) custom-call(s32[192,8]{1,0:T(8,128)} %copy.14.ids_ref, f32[1,1024]{1,0:T(1,128)} %bitcast.1, bf16[192,2048]{1,0:T(8,128)(2,1)} %q_in.1, bf16[192,2048]{1,0:T(8,128)(2,1)} %k_in.1, bf16[192,2048]{1,0:T(8,128)(2,1)} %v_in.1, ...), custom_call_target="tpu_custom_call" | custom-call | tf_op jit(solution)/shard_map/pallas_call | solution.py:611
  126.7 1.7 %fusion = f32[48,8]{0,1:T(8,128)} fusion(f32[192,128]{1,0:T(8,128)} %get-tuple-element.8, s32[48]{0:T(128)S(1)} %dynamic_slice.3), kind=kOutput, calls=%fused_computation | convolution fusion | flops 893952 | bytes 100032 | tf_op jit(solution)/shard_map/dot_general | solution.py:675
  128.4 2.1 %copy.18 = bf16[192,2048]{1,0:T(8,128)(2,1)} copy(bf16[192,2048]{1,0:T(8,128)(2,1)} %get-tuple-element.17) | data formatting | bytes 1572864
  130.5 2.1 %copy.19 = bf16[192,2048]{1,0:T(8,128)(2,1)} copy(bf16[192,2048]{1,0:T(8,128)(2,1)} %get-tuple-element.18) | data formatting | bytes 1572864
  132.6 2.1 %copy.20 = bf16[192,2048]{1,0:T(8,128)(2,1)} copy(bf16[192,2048]{1,0:T(8,128)(2,1)} %get-tuple-element.19) | data formatting | bytes 1572864
where the time goes:
time: 135 us
  Pallas kernels  124 us (92%)
  local copies, waits for them, and re-layouts  7.79 us (6%)
  matrix products  1.74 us (1%)
    pallas_call x1, Pallas kernels, fused_shards(): pl.pallas_call(functools.partial(fused_kernel, seq_count, grp_count), out...  124 us
    unnamed x4, local copies, waits for them, and re-layouts  7.71 us

commit v1 on v0

v1 whole, which is shorter than its diff:
```python
import functools

import jax
import jax.numpy as jnp
from jax import lax
from jax.experimental import pallas as pl
from jax.experimental.pallas import tpu as pltpu
from jax.sharding import PartitionSpec as P

HEAD = 128
PATCH = 8


EPSILON = 1e-05
FLOOR = -1e30


def shortened(value):
    return jax.tree.map(lambda a: a.astype(jnp.bfloat16) if a.dtype == jnp.float32 else a, value)


def partner_2(value, axis, bit):
    mask = 2**bit
    pairs = [(source, source ^ mask) for source in range(lax.axis_size(axis))]
    return lax.ppermute(value, axis, pairs)


def local_model(context, byte_ids, byte_embed, norm_gain, w_up, w_down, vocab_head):
    patch_count = context.shape[0]
    model_width = byte_embed.shape[1]
    vocab_size = vocab_head.shape[1]
    hidden_in = context.astype(jnp.float32).reshape(patch_count * PATCH, model_width)
    previous = jnp.concatenate([byte_ids[:, :1], byte_ids[:, :-1]], axis=1).reshape(-1)
    live_rows = jnp.tile(jnp.arange(PATCH) > 0, patch_count)
    letters = jnp.arange(vocab_size)
    one_hot = ((previous[:, None] == letters[None, :]) & live_rows[:, None]).astype(jnp.bfloat16)
    hidden_in = hidden_in + jnp.dot(one_hot, byte_embed, preferred_element_type=jnp.float32)
    inverse_rms = lax.rsqrt(jnp.mean(hidden_in * hidden_in, axis=1, keepdims=True) + EPSILON)
    normed = (hidden_in * inverse_rms * norm_gain).astype(jnp.bfloat16)
    raised = jnp.dot(normed, w_up, preferred_element_type=jnp.float32)
    active = jax.nn.gelu(raised, approximate=True).astype(jnp.bfloat16)
    after_mlp = hidden_in + jnp.dot(active, w_down, preferred_element_type=jnp.float32)
    final_scale = lax.rsqrt(jnp.mean(after_mlp * after_mlp, axis=1, keepdims=True) + EPSILON)
    final_rows = (after_mlp * final_scale).astype(jnp.bfloat16)
    logits = jnp.dot(final_rows, vocab_head, preferred_element_type=jnp.float32)
    row_top = lax.stop_gradient(jnp.max(logits, axis=1, keepdims=True))
    log_total = jnp.log(jnp.sum(jnp.exp(logits - row_top), axis=1)) + row_top[:, 0]
    target = byte_ids.reshape(-1)
    chosen = jnp.sum(jnp.where(target[:, None] == letters[None, :], logits, 0.0), axis=1)
    return (log_total - chosen).reshape(patch_count, PATCH)


def head_order(flat, head_count, segments, seq_count):
    row_total = flat.shape[0]
    block_rows = row_total // segments
    arranged = flat.reshape(block_rows, segments, head_count, HEAD).transpose(2, 1, 0, 3)
    return arranged.reshape(seq_count, -1, block_rows, HEAD)


def row_order(stack, head_count, segments):
    block_rows = stack.shape[2]
    arranged = stack.reshape(head_count, segments, block_rows, HEAD).transpose(2, 1, 0, 3)
    return arranged.reshape(block_rows * segments, head_count * HEAD)


def shards(
    byte_ids,
    patch_order,
    query_rows,
    key_rows,
    value_rows,
    byte_embed,
    norm_gain,
    w_up,
    w_down,
    vocab_head,
):
    row_count = query_rows.shape[0]
    head_count = query_rows.shape[1] // HEAD
    seq_here = lax.axis_index("seq")
    grp_here = lax.axis_index("grp")
    first_here = seq_here * row_count
    seq_count = lax.axis_size("seq")
    segments = max(1, seq_count // head_count)
    held_heads = max(1, head_count // seq_count)
    bit_count = segments.bit_length() - 1
    residue = seq_here % segments
    arranged = tuple(
        (
            head_order(member, head_count, segments, seq_count)
            for member in (query_rows, key_rows, value_rows)
        )
    )
    own_query, own_key, own_value = jax.tree.map(
        lambda part, own: part.astype(own.dtype),
        lax.all_to_all(shortened(arranged), "seq", split_axis=0, concat_axis=2, tiled=True),
        arranged,
    )
    stacked = jnp.stack([own_key, own_value])
    for bit in range(bit_count):
        partner = partner_2(shortened(stacked), "seq", bit).astype(stacked.dtype)
        upper_half = seq_here >> bit & 1 == 1
        stacked = jnp.where(
            upper_half,
            jnp.concatenate([partner, stacked], 1),
            jnp.concatenate([stacked, partner], 1),
        )
    slot_count = own_query.shape[2]
    full_pairs = stacked.transpose(0, 2, 3, 1, 4).reshape(
        2, held_heads, slot_count * segments, HEAD
    )
    full_key = full_pairs[0]
    full_value = full_pairs[1]
    head_queries = own_query[0]
    query_pos = jnp.arange(slot_count, dtype=jnp.int32) * segments + residue
    key_pos = jnp.arange(slot_count * segments, dtype=jnp.int32)
    allowed = (key_pos[None, :] <= query_pos[:, None])[None]
    scores = jnp.einsum(
        "hqd,hkd->hqk", head_queries, full_key, preferred_element_type=jnp.float32
    ) * HEAD ** (-0.5)
    row_top = jnp.max(jnp.where(allowed, scores, FLOOR), axis=2, keepdims=True)
    spread = jnp.where(allowed, jnp.exp(jnp.where(allowed, scores - row_top, FLOOR)), 0.0)
    head_mass = row_top[:, :, 0] + jnp.log(jnp.sum(spread, axis=2))
    chances = jnp.where(
        allowed, jnp.exp(jnp.where(allowed, scores - head_mass[:, :, None], FLOOR)), 0.0
    )
    rounded_weights = chances.astype(jnp.bfloat16)
    head_attended = jnp.einsum(
        "hqk,hkd->hqd", chances, full_value.astype(jnp.float32), precision=lax.Precision.HIGHEST
    ).astype(jnp.bfloat16)
    attended = row_order(
        lax.all_to_all(head_attended[None], "seq", split_axis=2, concat_axis=0, tiled=True),
        head_count,
        segments,
    )
    local_order = patch_order - first_here
    ordered = jnp.take(attended, local_order, axis=0)
    owned_rows = lax.all_to_all(ordered, "grp", split_axis=0, concat_axis=1, tiled=True)
    group_rows = owned_rows.shape[0]
    slot_patches = lax.dynamic_slice_in_dim(local_order, grp_here * group_rows, group_rows, 0)
    slot_bytes = jnp.take(byte_ids, slot_patches, axis=0)

    def scored(context):
        return local_model(context, slot_bytes, byte_embed, norm_gain, w_up, w_down, vocab_head)

    byte_loss, pull_back = jax.vjp(scored, owned_rows)
    (context_grad,) = pull_back(jnp.ones_like(byte_loss))
    returned = lax.all_to_all(context_grad, "grp", split_axis=1, concat_axis=0, tiled=True)
    grads_flat = jnp.zeros_like(returned).at[local_order].set(returned)
    arranged_grads = head_order(grads_flat, head_count, segments, seq_count)
    grad_heads = lax.all_to_all(arranged_grads, "seq", split_axis=0, concat_axis=2, tiled=True)[0]
    head_dot = jnp.sum(grad_heads.astype(jnp.float32) * head_attended.astype(jnp.float32), axis=2)
    chance_grad = jnp.einsum(
        "hqd,hkd->hqk", grad_heads, full_value, preferred_element_type=jnp.float32
    )
    score_grad = (chances * (chance_grad - head_dot[:, :, None])).astype(jnp.bfloat16)
    query_heads = (
        jnp.einsum("hqk,hkd->hqd", score_grad, full_key, preferred_element_type=jnp.float32)
        * HEAD ** (-0.5)
    ).astype(jnp.bfloat16)
    key_part = jnp.einsum(
        "hqk,hqd->hkd", score_grad, head_queries, preferred_element_type=jnp.float32
    ) * HEAD ** (-0.5)
    value_part = jnp.einsum(
        "hqk,hqd->hkd", rounded_weights, grad_heads, preferred_element_type=jnp.float32
    )
    partial_pairs = (
        jnp.stack([key_part, value_part])
        .reshape(2, held_heads, slot_count, segments, HEAD)
        .transpose(0, 3, 1, 2, 4)
    )
    for bit in reversed(range(bit_count)):
        half_count = partial_pairs.shape[1] // 2
        upper_half = seq_here >> bit & 1 == 1
        lower_part = partial_pairs[:, :half_count]
        upper_part = partial_pairs[:, half_count:]
        kept_half = jnp.where(upper_half, upper_part, lower_part)
        sent_half = jnp.where(upper_half, lower_part, upper_part)
        partial_pairs = kept_half + partner_2(sent_half.astype(jnp.bfloat16), "seq", bit).astype(
            sent_half.dtype
        )
    key_heads = partial_pairs[0].astype(jnp.bfloat16)
    value_heads = partial_pairs[1].astype(jnp.bfloat16)
    back_query, back_key, back_value = (
        lax.all_to_all(query_heads[None], "seq", split_axis=2, concat_axis=0, tiled=True),
        lax.all_to_all(key_heads, "seq", split_axis=2, concat_axis=0, tiled=True),
        lax.all_to_all(value_heads, "seq", split_axis=2, concat_axis=0, tiled=True),
    )
    query_out = row_order(back_query, head_count, segments)
    key_out = row_order(back_key, head_count, segments)
    value_out = row_order(back_value, head_count, segments)
    return (byte_loss, query_out, key_out, value_out)


MESH = pl.DeviceIdType.MESH
LANES = 128
KEY_TILE = 256
HIDDEN_TILE = 1024
GELU_A = 0.7978845608028654
GELU_B = 0.044715
LOG2E = 1.4426950408889634
SCALE = HEAD ** (-0.5)


def dot_nn(a, b):
    return lax.dot_general(a, b, (((1,), (0,)), ((), ())), preferred_element_type=jnp.float32)


def dot_nt(a, b):
    return lax.dot_general(a, b, (((1,), (1,)), ((), ())), preferred_element_type=jnp.float32)


def dot_tn(a, b):
    return lax.dot_general(a, b, (((0,), (0,)), ((), ())), preferred_element_type=jnp.float32)


def dot_exact(a, b, dims):
    return lax.dot_general(
        a, b, (dims, ((), ())), precision=lax.Precision.HIGHEST, preferred_element_type=jnp.float32
    )


def fused_kernel(
    seq_count,
    grp_count,
    ids_in,
    order_in,
    gain_in,
    q_in,
    k_in,
    v_in,
    embed_in,
    up_in,
    down_in,
    vocab_in,
    loss_out,
    dq_out,
    dk_out,
    dv_out,
    q_buf,
    k_buf,
    v_buf,
    p_buf,
    att,
    ctx,
    dctx,
    dout,
    dq_buf,
    dk_buf,
    dv_buf,
    q_turned,
    g_turned,
    embed,
    up,
    down,
    up_turned,
    down_turned,
    vocab,
    ids,
    order,
    gain,
    hid,
    normed,
    slope,
    acc,
    dafter,
    dafter_low,
    losses,
    in_recv,
    in_send,
    weight_sem,
    ctx_recv,
    ctx_send,
    grad_recv,
    grad_send,
    loss_recv,
    loss_send,
    out_recv,
    out_send,
):
    me_s = lax.axis_index("seq")
    me_g = lax.axis_index("grp")
    jobs, total, _ = q_buf.shape
    rows = total // seq_count
    part = rows // grp_count
    model = embed.shape[1]
    vocab_size = embed.shape[0]
    ffl = up.shape[1]

    barrier = pltpu.get_barrier_semaphore()

    def greet_seq(d, _):
        peer = lax.rem(me_s + d, seq_count)
        pl.semaphore_signal(barrier, inc=1, device_id=(peer, me_g), device_id_type=MESH)
        return 0

    def greet_grp(d, _):
        peer = lax.rem(me_g + d, grp_count)
        pl.semaphore_signal(barrier, inc=1, device_id=(me_s, peer), device_id_type=MESH)
        return 0

    lax.fori_loop(1, grp_count, greet_grp, 0)
    lax.fori_loop(1, seq_count, greet_seq, 0)

    weight_copies = [
        pltpu.make_async_copy(a, b, weight_sem.at[n])
        for n, (a, b) in enumerate(
            (
                (ids_in, ids),
                (embed_in, embed),
                (gain_in, gain),
                (vocab_in, vocab),
                (up_in, up),
                (down_in, down),
                (order_in, order),
            )
        )
    ]
    for copy in weight_copies:
        copy.start()

    def block_of(index, size):
        return pl.ds(pl.multiple_of(index * size, size), size)

    def out_cols(job, owner):
        return block_of(job * seq_count + owner, HEAD)

    my_rows = block_of(me_s, rows)
    my_head = block_of(me_s, HEAD)
    arrays = ((k_in, k_buf), (q_in, q_buf), (v_in, v_buf))
    for job in range(jobs):
        for n, (source, target) in enumerate(arrays):
            pltpu.make_async_copy(
                source.at[:, out_cols(job, me_s)], target.at[job, my_rows], in_recv.at[job, n]
            ).start()
    pl.semaphore_wait(barrier, seq_count - 1 + grp_count - 1)

    whole = pl.ds(0, rows)
    halves = (pl.ds(0, rows // 2), pl.ds(rows // 2, rows // 2))

    def send_in(job, n, piece=whole):
        source, target = arrays[n]
        there = pl.ds(pl.multiple_of(me_s * rows + piece.start, piece.size), piece.size)

        def send_one(d, _):
            peer = lax.rem(me_s + d, seq_count)
            pltpu.make_async_remote_copy(
                src_ref=source.at[piece, out_cols(job, peer)],
                dst_ref=target.at[job, there],
                send_sem=in_send.at[n],
                recv_sem=in_recv.at[job, n],
                device_id=(peer, me_g),
                device_id_type=MESH,
            ).start()
            return 0

        lax.fori_loop(1, seq_count, send_one, 0)

    def wait_in(job, n):
        target = arrays[n][1].at[job]
        pltpu.make_async_copy(target, target, in_recv.at[job, n]).wait()

    widths = [-(-((i + 1) * rows) // KEY_TILE) * KEY_TILE for i in range(seq_count)]

    def letters_hot(t):
        letters = lax.broadcasted_iota(jnp.int32, (vocab_size, rows), 0)
        return letters == ids[pl.ds(t, 1), :]

    def embed_bytes(job):
        byte = me_g * jobs + job
        hot = letters_hot(jnp.maximum(byte - 1, 0)) & (byte > 0)
        hid[job] = dot_tn(hot.astype(jnp.bfloat16), embed[...])

    def weigh(job):
        for i, w in enumerate(widths):
            start = i * rows // LANES * LANES
            s = dot_nt(q_buf[job, i * rows : (i + 1) * rows], k_buf[job, :w])
            tail = s[:, start:]
            key_pos = lax.broadcasted_iota(jnp.int32, tail.shape, 1) + start
            query_pos = lax.broadcasted_iota(jnp.int32, tail.shape, 0) + i * rows
            tail = jnp.where(key_pos <= query_pos, tail, FLOOR)
            if start:
                s = jnp.concatenate([s[:, :start], tail], axis=1)
            else:
                s = tail
            top = jnp.max(s, axis=1, keepdims=True)
            e = jnp.exp2((s - top) * (SCALE * LOG2E))
            inverse = 1.0 / jnp.sum(e, axis=1, keepdims=True)
            p_buf[job, i * rows : (i + 1) * rows, :w] = (e * inverse).astype(jnp.bfloat16)

    def turn(source, target):
        for c in range(total // KEY_TILE):
            here = slice(c * KEY_TILE, (c + 1) * KEY_TILE)
            target[:, here] = source[here, :].astype(jnp.float32).T.astype(jnp.bfloat16)

    def turn_weights():
        def turn_chunk(c, _):
            chunk = block_of(c, KEY_TILE)
            for k in range(model // KEY_TILE):
                here = slice(k * KEY_TILE, (k + 1) * KEY_TILE)
                up_turned[chunk, here] = up[here, chunk].T
                down_turned[here, chunk] = down[chunk, here].T
            return 0

        lax.fori_loop(0, ffl // KEY_TILE, turn_chunk, 0)

    def attend(job):
        def send_ctx(i):
            @pl.when(me_s != i)
            def _():
                pltpu.make_async_remote_copy(
                    src_ref=att.at[job, i * rows : (i + 1) * rows],
                    dst_ref=ctx.at[job, :, my_head],
                    send_sem=ctx_send,
                    recv_sem=ctx_recv.at[job],
                    device_id=(i, me_g),
                    device_id_type=MESH,
                ).start()

        for i, w in enumerate(widths):
            here = slice(i * rows, (i + 1) * rows)
            att[job, here] = dot_nn(p_buf[job, here, :w], v_buf[job, :w]).astype(jnp.bfloat16)
            if i:
                send_ctx(i - 1)
        ctx[job, :, my_head] = att[job, my_rows]
        send_ctx(seq_count - 1)

    def byte_model(job):
        others = ctx.at[job, :, : (seq_count - 1) * HEAD]
        pltpu.make_async_copy(others, others, ctx_recv.at[job]).wait()
        h0 = hid[job] + ctx[job].astype(jnp.float32)
        hid[job] = h0
        inverse_rms = lax.rsqrt(jnp.mean(h0 * h0, axis=1, keepdims=True) + EPSILON)
        normed[...] = (h0 * inverse_rms * gain[...]).astype(jnp.bfloat16)
        acc[...] = h0

        for c in range(ffl // HIDDEN_TILE):
            chunk = slice(c * HIDDEN_TILE, (c + 1) * HIDDEN_TILE)
            x = dot_nn(normed[...], up[:, chunk])
            square = x * x
            th = jnp.tanh(x * (GELU_A + (GELU_A * GELU_B) * square))
            half = 0.5 + 0.5 * th
            active = (x * half).astype(jnp.bfloat16)
            slope[:, chunk] = half + (0.5 * x) * (1.0 - th * th) * (
                GELU_A + (3.0 * GELU_A * GELU_B) * square
            )
            acc[...] += dot_nn(active, down[chunk, :])
        after = acc[...]
        final_scale = lax.rsqrt(jnp.mean(after * after, axis=1, keepdims=True) + EPSILON)
        final_rows = (after * final_scale).astype(jnp.bfloat16)
        logits = dot_nn(final_rows, vocab[...])
        top = jnp.max(logits, axis=1, keepdims=True)
        e = jnp.exp(logits - top)
        z = jnp.sum(e, axis=1, keepdims=True)
        byte = me_g * jobs + job
        same = lax.broadcasted_iota(jnp.int32, (vocab_size, vocab_size), 0)
        same = same == lax.broadcasted_iota(jnp.int32, (vocab_size, vocab_size), 1)
        hot = dot_tn(letters_hot(byte).astype(jnp.bfloat16), same.astype(jnp.bfloat16))
        loss = jnp.log(z) + top - jnp.sum(hot * logits, axis=1, keepdims=True)
        lane = lax.broadcasted_iota(jnp.int32, (rows, LANES), 1)
        before = losses[me_g] if job else jnp.zeros((rows, LANES), jnp.float32)
        losses[me_g] = jnp.where(lane == byte, loss, before)
        dlogits = (e / z - hot).astype(jnp.bfloat16)
        dfinal = dot_nt(dlogits, vocab[...]).astype(jnp.bfloat16).astype(jnp.float32)
        after = acc[...]
        share = jnp.mean(dfinal * after, axis=1, keepdims=True)
        da = final_scale * dfinal - after * (final_scale * final_scale * final_scale * share)
        dafter[...] = da
        dafter_low[...] = da.astype(jnp.bfloat16)
        acc[...] = jnp.zeros_like(acc)

        for c in range(ffl // HIDDEN_TILE):
            chunk = slice(c * HIDDEN_TILE, (c + 1) * HIDDEN_TILE)
            dactive = dot_nn(dafter_low[...], down_turned[:, chunk]).astype(jnp.bfloat16)
            draised = (dactive.astype(jnp.float32) * slope[:, chunk]).astype(jnp.bfloat16)
            acc[...] += dot_nn(draised, up_turned[chunk, :])
        dn = acc[...].astype(jnp.bfloat16).astype(jnp.float32) * gain[...]
        h0 = hid[job]
        share = jnp.mean(dn * h0, axis=1, keepdims=True)
        dh = inverse_rms * dn - h0 * (inverse_rms * inverse_rms * inverse_rms * share)
        dctx[job] = (dh + dafter[...]).astype(jnp.bfloat16)
        dout[job, my_rows] = dctx[job, :, my_head]

        def send_grad(d, _):
            peer = lax.rem(me_s + d, seq_count)
            pltpu.make_async_remote_copy(
                src_ref=dctx.at[job, :, block_of(peer, HEAD)],
                dst_ref=dout.at[job, my_rows],
                send_sem=grad_send,
                recv_sem=grad_recv.at[job],
                device_id=(peer, me_g),
                device_id_type=MESH,
            ).start()
            return 0

        lax.fori_loop(1, seq_count, send_grad, 0)

    def send_losses():
        def send_loss(d, _):
            pltpu.make_async_remote_copy(
                src_ref=losses.at[me_g],
                dst_ref=losses.at[me_g],
                send_sem=loss_send,
                recv_sem=loss_recv,
                device_id=(me_s, lax.rem(me_g + d, grp_count)),
                device_id_type=MESH,
            ).start()
            return 0

        lax.fori_loop(1, grp_count, send_loss, 0)

    def send_out(job, n, i, source, target, piece=whole):
        here = source.at[job, pl.ds(i * rows + piece.start, piece.size)]
        there = target.at[piece, out_cols(job, me_s)]

        @pl.when(me_s != i)
        def _():
            pltpu.make_async_remote_copy(
                src_ref=here,
                dst_ref=there,
                send_sem=out_send.at[n],
                recv_sem=out_recv.at[n],
                device_id=(i, me_g),
                device_id_type=MESH,
            ).start()

        @pl.when(me_s == i)
        def _():
            pltpu.make_async_copy(here, there, out_recv.at[n]).start()

    firsts = [
        next(i for i, w in enumerate(widths) if w >= (c + 1) * KEY_TILE) * rows
        for c in range(total // KEY_TILE)
    ]

    def clear_edges():
        for c, first in enumerate(firsts):
            if first % LANES:
                above = slice(first // LANES * LANES, first)
                here = slice(c * KEY_TILE, (c + 1) * KEY_TILE)
                p_buf[:, above, here] = jnp.zeros((jobs, first % LANES, KEY_TILE), jnp.bfloat16)

    def key_side(job, turned, matrix, result, factor):
        for c in range(total // KEY_TILE):
            first = firsts[c] // LANES * LANES
            here = slice(c * KEY_TILE, (c + 1) * KEY_TILE)
            block = dot_nn(turned[:, first:], matrix[first:, here])
            if factor is not None:
                block = block * factor
            result[job, here] = block.T.astype(jnp.bfloat16)

    def send_keys(job, piece):
        for i in range(seq_count):
            send_out(job, 1, i, dk_buf, dk_out, piece)

    def value_side(job):
        turn(dout.at[job], g_turned)
        key_side(job, g_turned, p_buf.at[job], dv_buf, None)
        for i in range(seq_count):
            send_out(job, 2, i, dv_buf, dv_out)

    def query_side(job, kept):
        for i, w in enumerate(widths):
            here = slice(i * rows, (i + 1) * rows)
            g = dout[job, here]
            row_dot = jnp.sum(
                g.astype(jnp.float32) * att[job, here].astype(jnp.float32), axis=1, keepdims=True
            )
            dp = dot_nt(g, v_buf[job, :w])
            ds = (p_buf[job, here, :w].astype(jnp.float32) * (dp - row_dot)).astype(jnp.bfloat16)
            kept[here, :w] = ds
            dq_buf[job, here] = (dot_nn(ds, k_buf[job, :w]) * SCALE).astype(jnp.bfloat16)
            if i:
                send_out(job, 0, i - 1, dq_buf, dq_out)
        send_out(job, 0, seq_count - 1, dq_buf, dq_out)

    def wait_grad(job):
        others = dout.at[job, : (seq_count - 1) * rows]
        pltpu.make_async_copy(others, others, grad_recv.at[job]).wait()

    def attend_back(job):
        wait_grad(job)
        value_side(job)
        query_side(job, p_buf.at[job])
        key_side(job, q_turned.at[job], p_buf.at[job], dk_buf, SCALE)
        send_keys(job, halves[0])

    def attend_back_last(job):
        wait_grad(job)
        query_side(job, p_buf.at[job - 1])
        value_side(job)
        key_side(job, q_turned.at[job], p_buf.at[job - 1], dk_buf, SCALE)
        send_keys(job, whole)

    def attend_fore(job):
        wait_in(job, 0)
        wait_in(job, 1)
        weigh(job)
        turn(q_buf.at[job], q_turned.at[job])
        wait_in(job, 2)
        attend(job)

    send_in(0, 0)
    send_in(0, 1)
    send_in(0, 2)
    send_in(1, 0, halves[0])
    clear_edges()
    for copy in weight_copies[:3]:
        copy.wait()
    for job in range(jobs):
        embed_bytes(job)
    for copy in weight_copies[3:]:
        copy.wait()
    turn_weights()
    attend_fore(0)
    send_in(1, 0, halves[1])
    send_in(1, 1)
    send_in(1, 2)
    for job in range(2, jobs):
        for n in range(3):
            send_in(job, n)
    byte_model(0)
    for job in range(1, jobs):
        attend_fore(job)
        attend_back(job - 1)
        byte_model(job)
        send_keys(job - 1, halves[1])
    send_losses()
    attend_back_last(jobs - 1)

    loss_others = losses.at[: grp_count - 1]
    pltpu.make_async_copy(loss_others, loss_others, loss_recv).wait()
    every = losses[0]
    for g in range(1, grp_count):
        every = every + losses[g]
    patches = lax.broadcasted_iota(jnp.int32, (rows, rows), 0)
    taken = (patches == order[...] - me_s * rows).astype(jnp.float32)
    by_slot = dot_exact(every, taken, ((0,), (0,)))[:PATCH]
    slots = lax.broadcasted_iota(jnp.int32, (rows, part), 0)
    mine = slots == lax.broadcasted_iota(jnp.int32, (rows, part), 1) + me_g * part
    loss_out[...] = dot_exact(by_slot, mine.astype(jnp.float32), ((1,), (0,)))

    pltpu.make_async_copy(loss_others, loss_others, loss_send).wait()
    sent = q_in.at[:, : (seq_count - 1) * jobs * HEAD]
    for n in range(3):
        pltpu.make_async_copy(sent, sent, in_send.at[n]).wait()
    others = ctx.at[:, :, : (seq_count - 1) * HEAD]
    pltpu.make_async_copy(others, others, ctx_send).wait()
    pltpu.make_async_copy(others, others, grad_send).wait()
    for n, target in enumerate((dq_out, dk_out, dv_out)):
        pltpu.make_async_copy(target, target, out_recv.at[n]).wait()
        pltpu.make_async_copy(sent, sent, out_send.at[n]).wait()


def fits(seq_count, grp_count, byte_ids, patch_order, query_rows, *rest):
    rows, columns = query_rows.shape
    vocab_size, model = rest[2].shape
    ffl = rest[4].shape[1]
    total = rows * seq_count
    return (
        PATCH % grp_count == 0
        and PATCH // grp_count >= 2
        and seq_count * HEAD == model
        and columns == PATCH // grp_count * model
        and rows % (16 * grp_count) == 0
        and rows // grp_count <= LANES
        and vocab_size % LANES == 0
        and total % KEY_TILE == 0
        and ffl % HIDDEN_TILE == 0
        and model % KEY_TILE == 0
        and PATCH // grp_count * total * total <= 6 * 1024 * 1024
    )


def fused_shards(
    seq_count,
    grp_count,
    byte_ids,
    patch_order,
    query_rows,
    key_rows,
    value_rows,
    byte_embed,
    norm_gain,
    w_up,
    w_down,
    vocab_head,
):
    rows, columns = query_rows.shape
    jobs = PATCH // grp_count
    total = rows * seq_count
    part = rows // grp_count
    vocab_size, model = byte_embed.shape
    ffl = w_up.shape[1]
    low, wide = jnp.bfloat16, jnp.float32
    anywhere = pl.BlockSpec(memory_space=pl.ANY)
    dma = pltpu.SemaphoreType.DMA
    by_job = [pltpu.VMEM((jobs, total, HEAD), low)] * 3
    losses, query_grad, key_grad, value_grad = pl.pallas_call(
        functools.partial(fused_kernel, seq_count, grp_count),
        out_shape=(pltpu.VMEM((PATCH, part), wide), *[pltpu.VMEM((rows, columns), low)] * 3),
        in_specs=[anywhere] * 10,
        out_specs=(pl.BlockSpec(memory_space=pltpu.VMEM), anywhere, anywhere, anywhere),
        scratch_shapes=[
            *by_job,
            pltpu.VMEM((jobs, total, total), low),
            pltpu.VMEM((jobs, total, HEAD), low),
            pltpu.VMEM((jobs, rows, model), low),
            pltpu.VMEM((jobs, rows, model), low),
            pltpu.VMEM((jobs, total, HEAD), low),
            *by_job,
            pltpu.VMEM((jobs, HEAD, total), low),
            pltpu.VMEM((HEAD, total), low),
            pltpu.VMEM((vocab_size, model), low),
            pltpu.VMEM((model, ffl), low),
            pltpu.VMEM((ffl, model), low),
            pltpu.VMEM((ffl, model), low),
            pltpu.VMEM((model, ffl), low),
            pltpu.VMEM((model, vocab_size), low),
            pltpu.VMEM((PATCH, rows), jnp.int32),
            pltpu.VMEM((1, rows), jnp.int32),
            pltpu.VMEM((1, model), wide),
            pltpu.VMEM((jobs, rows, model), wide),
            pltpu.VMEM((rows, model), low),
            pltpu.VMEM((rows, ffl), wide),
            pltpu.VMEM((rows, model), wide),
            pltpu.VMEM((rows, model), wide),
            pltpu.VMEM((rows, model), low),
            pltpu.VMEM((grp_count, rows, LANES), wide),
            dma((jobs, 3)),
            dma((3,)),
            dma((7,)),
            dma((jobs,)),
            dma,
            dma((jobs,)),
            dma,
            dma,
            dma,
            dma((3,)),
            dma((3,)),
        ],
        compiler_params=pltpu.CompilerParams(
            collective_id=0, has_side_effects=True, vmem_limit_bytes=64_000_000
        ),
    )(
        byte_ids.T,
        patch_order.reshape(1, rows),
        norm_gain.reshape(1, model),
        query_rows,
        key_rows,
        value_rows,
        byte_embed,
        w_up,
        w_down,
        vocab_head,
    )
    return losses.T, query_grad, key_grad, value_grad


def solution(mesh):
    placed = (
        P("seq", None),
        P("seq"),
        P("seq", "grp"),
        P("seq", "grp"),
        P("seq", "grp"),
        P(),
        P(),
        P(),
        P(),
        P(),
    )
    seq_count, grp_count = mesh.shape["seq"], mesh.shape["grp"]

    def body(*args):
        if fits(seq_count, grp_count, *args):
            return fused_shards(seq_count, grp_count, *args)
        return shards(*args)

    return jax.shard_map(
        body,
        mesh=mesh,
        in_specs=placed,
        out_specs=(P(("seq", "grp"), None), P("seq", "grp"), P("seq", "grp"), P("seq", "grp")),
        check_vma=False,
    )
```

time: 135 us -> 85 us (0.63)
  Pallas kernels: 124 us -> 80.5 us
  local copies, waits for them, and re-layouts: 7.79 us -> 3.23 us
  matrix products: 1.74 us -> 0 us
    pallas_call x1, Pallas kernels: 124 us -> 80.5 us  [fused_shards(): pl.pallas_call(functools.partial(fused_kernel, seq_count, grp_count), out...]
    unnamed x4, local copies, waits for them, and re-layouts: 7.71 us -> 3.23 us
    dot_general x1 -> x0, matrix products: 1.74 us -> none  [fused_shards(): jnp.dot(chosen, losses, precision=lax.Precision.HIGHEST)[:, :PATCH]]
where the time goes in v1:
time: 85 us; the launch traced here: 84.4 us
  Pallas kernels  80.5 us (95%)
  local copies, waits for them, and re-layouts  3.23 us (4%)
    pallas_call x1, Pallas kernels, fused_shards(): pl.pallas_call(functools.partial(fused_kernel, seq_count, grp_count), out...  80.5 us
    unnamed x4, local copies, waits for them, and re-layouts  3.23 us

profile of v1, /device:TPU:1, one launch (start us, length us, event | category | flops | bytes accessed | tf_op | source)
XLA Modules:
  0.0 84.4 jit_solution(9882145351222923129)
XLA Ops:
  0.6 80.5 %shard_map.129 = (f32[8,48]{1,0:T(8,128)S(1)}, bf16[192,2048]{1,0:T(8,128)(2,1)S(1)}, bf16[192,2048]{1,0:T(8,128)(2,1)S(1)}, bf16[192,2048]{1,0:T(8,128)(2,1)S(1)}) custom-call(s32[8,192]{1,0:T(8,128)} %bitcast.5, s32[1,192]{1,0:T(1,128)} %bitcast.7, f32[1,1024]{1,0:T(1,128)} %bitcast.6, bf16[192,2048]{1,0:T(8,128)(2,1)} %q_in.1, bf16[192,2048]{1,0:T(8,128)(2,1)} %k_in.1, ...), custom_call_target="tpu_custom_call" | custom-call | tf_op jit(solution)/shard_map/pallas_call | solution.py:699
  81.1 0.6 copy.18
  81.7 0.9 %copy.19 = bf16[192,2048]{1,0:T(8,128)(2,1)} copy(bf16[192,2048]{1,0:T(8,128)(2,1)S(1)} %get-tuple-element.13) | data formatting | bytes 1572864
  82.6 0.9 %copy.20 = bf16[192,2048]{1,0:T(8,128)(2,1)} copy(bf16[192,2048]{1,0:T(8,128)(2,1)S(1)} %get-tuple-element.14) | data formatting | bytes 1572864
  83.5 0.9 %copy.21 = bf16[192,2048]{1,0:T(8,128)(2,1)} copy(bf16[192,2048]{1,0:T(8,128)(2,1)S(1)} %get-tuple-element.15) | data formatting | bytes 1572864
